TPU v7x, 32 devices: a whole 2x2x4 slice. The times are simulated.
32 devices in a mesh: row: 4 (over x, core), col: 8 (over z, y).
Axes of the slice: x: 2, y: 2, z: 4, core: 2. Of those that a mesh axis runs over, the one named last changes fastest.
Arguments:
- panel_rows: float32 [4096, 4096], P('row', 'col'), may hold values from -0.75 to 0.75
- owner_slot: int32 [8, 8], replicated, may hold values from -1 to 15, as said below
Outputs:
- packed: float32 [4, 16, 512, 512], P('row', 'col')
Inputs may be any that keep to these rules, and one draw needn't show every extreme that they name: For j <= i, owner_slot[i, j] is the position of tile (i, j) among the 16 positions of group i // 2; tiles of one group have distinct positions; entries above the diagonal are -1. Position p lies on the device of col index p // 2.
All inputs are finite; a program needn't handle non-finite values.
Results may differ from a plain program's by a relative error of at most 0.0003.
Values sent between devices are 32-bit elements; how exact they have to be, the bound alone decides.
A program may use at most 128 MiB of HBM per device.

v0:
```python
import jax
import jax.numpy as jnp
from jax import lax
from jax.sharding import PartitionSpec as P

BLOCK = 512


def slot_table(owner_slot, group_id, positions, per_group):
    blocks = owner_slot.shape[0]
    block_row = jnp.arange(blocks, dtype=jnp.int32)[:, None]
    block_col = jnp.arange(blocks, dtype=jnp.int32)[None, :]
    inside = (block_row // per_group == group_id) & (block_col <= block_row)
    wanted = jnp.arange(positions, dtype=jnp.int32)[:, None, None]
    matched = inside[None] & (owner_slot[None] == wanted)
    is_live = jnp.any(matched, axis=(1, 2))
    left_block = jnp.sum(jnp.where(matched, block_row[None], 0), axis=(1, 2))
    right_block = jnp.sum(jnp.where(matched, block_col[None], 0), axis=(1, 2))
    return (left_block, right_block, is_live)


def tile_products(tiles_all, lefts, rights, flags):

    def single(packed_item):
        left_one, right_one, flag = packed_item

        def compute():
            return lax.dot_general(
                tiles_all[left_one],
                tiles_all[right_one],
                (((1,), (1,)), ((), ())),
                precision=lax.Precision.HIGHEST,
                preferred_element_type=jnp.float32,
            )

        def blank():
            return jnp.zeros((BLOCK, BLOCK), jnp.float32)

        return lax.cond(flag, compute, blank)

    return lax.map(single, (lefts, rights, flags))


def body(panel_rows, owner_slot):
    rows_n = lax.axis_size("row")
    cols_n = lax.axis_size("col")
    slab_rows, inner_cols = panel_rows.shape
    per_group = slab_rows // BLOCK
    blocks = per_group * rows_n
    row_tiles = per_group * (blocks - per_group) + per_group * (per_group + 1) // 2
    slot_count = (row_tiles + cols_n - 1) // cols_n
    positions = cols_n * slot_count
    gathered = lax.all_gather(panel_rows, "row", axis=0, tiled=True)
    my_group = lax.axis_index("row")
    left_block, right_block, is_live = slot_table(owner_slot, my_group, positions, per_group)
    tiles_all = gathered.reshape(blocks, BLOCK, inner_cols)
    summed = lax.psum_scatter(
        tile_products(tiles_all, left_block, right_block, is_live),
        "col",
        scatter_dimension=0,
        tiled=True,
    )
    return summed[None]


def solution(mesh):
    placed = (P("row", "col"), P())
    return jax.shard_map(
        body, mesh=mesh, in_specs=placed, out_specs=P("row", "col", None, None), check_vma=False
    )
```

profile of v0, /device:TPU:0, one launch (start us, length us, event | category | flops | bytes accessed | tf_op | source)
XLA Modules:
  0.0 511.3 jit_solution(8440207610990684150)
XLA Ops:
  6.5 0.7 all-gather.2.cloned.1.call-update
  7.4 0.8 select_reduce_fusion
  8.2 0.8 fusion.6
  9.0 60.9 %all-gather.2.cloned.1.call-done = f32[4096,512]{1,0:T(8,128)} async-done(((f32[1024,512]{1,0:T(8,128)}), f32[4096,512]{1,0:T(8,128)}) %all-gather.2.cloned.1.call-update) | async-done | bytes 8388624 | tf_op jit(solution)/shard_map/all_gather | solution.py:53
  69.9 61.2 %while.10 = (s32[]{:T(128)}, f32[16,512,512]{2,1,0:T(8,128)}, pred[16]{0:T(512)(128)(4,1)S(1)}, s32[16]{0:T(128)S(1)}, f32[8,512,512]{2,1,0:T(8,128)}, /*index=5*/s32[16]{0:T(128)S(1)}, s32[]{:T(128)}) while((s32[]{:T(128)}, f32[16,512,512]{2,1,0:T(8,128)}, pred[16]{0:T(512)(128)(4,1)S(1)}, s32[16]{0:T(128)S(1)}, f32[8,512,512]{2,1,0:T(8,128)}, ...), condition=%wide.region_6.7_spmd, body=%wide.region_3.6_spmd.sunk | while | flops 1610612736 | bytes 5243620 | solution.py:41
  69.9 0.6 dynamic_slice.32
  71.2 1.1 constant_dynamic-update-slice_fusion.2
  72.3 0.6 dynamic_slice.32
  73.5 1.1 constant_dynamic-update-slice_fusion.2
  74.7 0.6 dynamic_slice.32
  75.8 7.9 %conditional.2 = (f32[1,512,512]{2,1,0:T(8,128)S(1)}) conditional(s32[]{:T(128)} %bitcast.14, () %tuple.31, (s32[16]{0:T(128)S(1)}, s32[]{:T(128)}, f32[8,512,512]{2,1,0:T(8,128)}, s32[16]{0:T(128)S(1)}) %tuple.32), branch_computations={%region_4.4_spmd, %region_5.5_spmd} | conditional | flops 1610612736 | bytes 3145836 | solution.py:39
  75.8 0.6 dynamic_slice.18
  78.1 0.6 dynamic_slice.20
  80.3 3.4 convolution_bitcast_fusion
  83.7 1.1 constant_dynamic-update-slice_fusion.2
  84.8 0.6 dynamic_slice.32
  86.1 1.1 constant_dynamic-update-slice_fusion.2
  87.1 0.6 dynamic_slice.32
  88.4 1.0 constant_dynamic-update-slice_fusion.2
  89.5 0.6 dynamic_slice.32
  90.8 1.1 constant_dynamic-update-slice_fusion.2
  91.9 0.6 dynamic_slice.32
  93.1 1.1 constant_dynamic-update-slice_fusion.2
  94.2 0.6 dynamic_slice.32
  95.5 1.0 constant_dynamic-update-slice_fusion.2
  96.6 0.6 dynamic_slice.32
  97.8 1.1 constant_dynamic-update-slice_fusion.2
  99.0 0.6 dynamic_slice.32
  100.3 1.0 constant_dynamic-update-slice_fusion.2
  101.3 0.6 dynamic_slice.32
  102.6 1.1 constant_dynamic-update-slice_fusion.2
  103.7 0.6 dynamic_slice.32
  104.9 1.0 constant_dynamic-update-slice_fusion.2
  106.0 0.6 dynamic_slice.32
  107.1 8.0 %conditional.2 = (f32[1,512,512]{2,1,0:T(8,128)S(1)}) conditional(s32[]{:T(128)} %bitcast.14, () %tuple.31, (s32[16]{0:T(128)S(1)}, s32[]{:T(128)}, f32[8,512,512]{2,1,0:T(8,128)}, s32[16]{0:T(128)S(1)}) %tuple.32), branch_computations={%region_4.4_spmd, %region_5.5_spmd} | conditional | flops 1610612736 | bytes 3145836 | solution.py:39
  107.2 0.6 dynamic_slice.18
  109.4 0.6 dynamic_slice.20
  111.7 3.4 convolution_bitcast_fusion
  115.1 1.1 constant_dynamic-update-slice_fusion.2
  116.2 0.6 dynamic_slice.32
  117.5 1.0 constant_dynamic-update-slice_fusion.2
  119.9 1.1 constant_dynamic-update-slice_fusion.2
  122.1 8.0 %conditional.2 = (f32[1,512,512]{2,1,0:T(8,128)S(1)}) conditional(s32[]{:T(128)} %bitcast.14, () %tuple.31, (s32[16]{0:T(128)S(1)}, s32[]{:T(128)}, f32[8,512,512]{2,1,0:T(8,128)}, s32[16]{0:T(128)S(1)}) %tuple.32), branch_computations={%region_4.4_spmd, %region_5.5_spmd} | conditional | flops 1610612736 | bytes 3145836 | solution.py:39
  122.1 0.6 dynamic_slice.18
  124.3 0.6 dynamic_slice.20
  126.6 3.5 convolution_bitcast_fusion
  130.1 1.1 constant_dynamic-update-slice_fusion.2
  131.2 373.2 %reduce-scatter.2.cloned.1.call-done = f32[2,512,512]{2,1,0:T(8,128)} async-done(((f32[16,512,512]{2,1,0:T(8,128)}), f32[2,512,512]{2,1,0:T(8,128)}) %reduce-scatter.2.cloned.1.call-update) | async-done | bytes 2097168 | tf_op jit(solution)/shard_map/reduce_scatter | solution.py:57
  (34 shorter events, 4.6 us)
Async XLA Ops:
  6.5 63.4 %all-gather.2.cloned.1.call-start = ((), (), s32[]{:S(2)}) async-start(), calls=%async_computation.1 | async-start | bytes 10485760 | tf_op jit(solution)/shard_map/all_gather | solution.py:53
  7.3 497.2 %reduce-scatter.2.cloned.1.call-start = ((), (), s32[]{:S(2)}) async-start(), calls=%async_computation.2 | async-start | bytes 18874368 | tf_op jit(solution)/shard_map/reduce_scatter | solution.py:57
Sparse Core Ops, SparseCore 0:
  8.9 60.9 all-gather.1
  131.3 373.0 reduce-scatter.1
where the time goes:
time: 513 us; the launch traced here: 511 us
  waiting for transfers between devices  435 us (85%)
  local copies, waits for them, and re-layouts  31.4 us (6%)
  loops' own time  19.6 us (4%)
  between operations  13.4 us (3%)
  matrix products  10.3 us (2%)
    reduce_scatter x1, waiting for transfers between devices, body(): lax.psum_scatter(tile_products(tiles_all, left_block, right_block, is_liv...  373 us
    all_gather x1, waiting for transfers between devices, body(): gathered = lax.all_gather(panel_rows, 'row', axis=0, tiled=True)  60.9 us
    dynamic_update_slice x16, local copies, waits for them, and re-layouts, tile_products(): return lax.map(single, (lefts, rights, flags))  17.1 us
    dynamic_slice x22, local copies, waits for them, and re-layouts, tile_products(): return lax.map(single, (lefts, rights, flags))  12.7 us
    another operation x16, loops' own time, single(): return lax.cond(flag, compute, blank)  10.4 us
    dot_general x3, matrix products, compute(): lax.dot_general(tiles_all[left_one], tiles_all[right_one], (((1,), (1,)),...  10.3 us
  transfers between devices with their start and end apart: 2, of which 2 were waited for; matrix products, arithmetic and copies ran while one was open for 0% of the time, Pallas kernels for 0%

commit v1 on v0

v1 whole, which is shorter than its diff:
```python
import functools

import jax
import jax.numpy as jnp
from jax import lax
from jax.experimental import pallas as pl
from jax.experimental.pallas import tpu as pltpu
from jax.sharding import PartitionSpec as P

BLOCK = 512
CHUNK = 256
MESH = pl.DeviceIdType.MESH
NT = (((1,), (1,)), ((), ()))


def slot_table(owner_slot, group_id, positions, per_group):
    blocks = owner_slot.shape[0]
    block_row = jnp.arange(blocks, dtype=jnp.int32)[:, None]
    block_col = jnp.arange(blocks, dtype=jnp.int32)[None, :]
    inside = (block_row // per_group == group_id) & (block_col <= block_row)
    wanted = jnp.arange(positions, dtype=jnp.int32)[:, None, None]
    matched = inside[None] & (owner_slot[None] == wanted)
    is_live = jnp.any(matched, axis=(1, 2))
    left_block = jnp.sum(jnp.where(matched, block_row[None], 0), axis=(1, 2))
    right_block = jnp.sum(jnp.where(matched, block_col[None], 0), axis=(1, 2))
    return (left_block, right_block, is_live)


def kernel(rows_n, cols_n, per_group, slots, table, panel, out, held, ysend, yrecv, zsend, zrecv, own,
           right_hi, right_lo, local_sem, load_recv, load_send, y_send, y_recv, z_send, z_recv):
    row, col = lax.axis_index("row"), lax.axis_index("col")
    chips = rows_n // 2
    far = cols_n // 4
    x, core = row // 2, row % 2
    h, low, y = col // 4, (col // 2) % 2, col % 2
    sibling = (row + 1 - 2 * core, col)
    pair = (row, h * 4 + (1 - low) * 2 + y)
    across = (row, h * 4 + low * 2 + 1 - y)
    beside = [(((x + d) % chips) * 2 + core, col) for d in range(1, chips)]
    ahead = [(row, ((h + d) % far) * 4 + low * 2 + y) for d in range(1, far)]
    partners = [sibling, pair, across] + beside + ahead

    fetch = pltpu.make_async_copy(panel, held.at[pl.ds(row * per_group, per_group), low], local_sem)
    fetch.start()
    barrier = pltpu.get_barrier_semaphore()
    for device in partners:
        pl.semaphore_signal(barrier, inc=1, device_id=device, device_id_type=MESH)
    pl.semaphore_wait(barrier, len(partners))
    fetch.wait()

    sent = []

    def piece(group, side, half):
        return held.at[group * per_group + half, side]

    def push(group, side, half, device):
        copy = pltpu.make_async_remote_copy(
            src_ref=piece(group, side, half),
            dst_ref=piece(group, side, half),
            send_sem=load_send.at[len(sent)],
            recv_sem=load_recv.at[group * per_group + half, side],
            device_id=device,
            device_id_type=MESH,
        )
        copy.start()
        sent.append(copy)

    def arrive(group, side, half):
        pltpu.make_async_remote_copy(
            src_ref=piece(group, side, half),
            dst_ref=piece(group, side, half),
            send_sem=load_send.at[0],
            recv_sem=load_recv.at[group * per_group + half, side],
            device_id=sibling,
            device_id_type=MESH,
        ).wait_recv()

    cut = per_group // 2
    ups, downs = list(range(cut)), list(range(cut, per_group))
    for half in ups + downs:
        for device in beside:
            push(row, low, half, device)
    for half in downs + ups:
        push(row, low, half, pair)
    for half in ups + downs:
        push(row, low, half, sibling)
    others = [((x + chips - d) % chips) * 2 + core for d in range(1, chips)]
    for group in others:
        for half in ups:
            arrive(group, low, half)
            push(group, low, half, pair)
            push(group, low, half, sibling)
    for half in downs:
        arrive(row, 1 - low, half)
        for device in beside:
            push(row, 1 - low, half, device)
        push(row, 1 - low, half, sibling)
    for group in others:
        for half in downs:
            arrive(group, low, half)
            push(group, low, half, sibling)
    for half in ups:
        arrive(row, 1 - low, half)
        push(row, 1 - low, half, sibling)
    for group in others:
        for half in ups + downs:
            arrive(group, 1 - low, half)
            push(group, 1 - low, half, sibling)
    for d in range(chips):
        group = ((x + d) % chips) * 2 + 1 - core
        for side in range(2):
            for half in range(per_group):
                arrive(group, side, half)

    depth = held.shape[-1]

    def tile(position, dst):
        left, right = table[0, position], table[1, position]
        for side in range(2):
            span = pl.ds(side * depth, depth)
            value = held[right, side]
            top = value.astype(jnp.bfloat16)
            right_hi[:, span] = top
            right_lo[:, span] = (value - top.astype(jnp.float32)).astype(jnp.bfloat16)

        @pl.loop(0, BLOCK // CHUNK)
        def _(step):
            rows = pl.ds(pl.multiple_of(step * CHUNK, CHUNK), CHUNK)
            total = jnp.zeros((CHUNK, BLOCK), jnp.float32)
            for side in range(2):
                span = pl.ds(side * depth, depth)
                value = held[left, side, rows, :]
                top = value.astype(jnp.bfloat16)
                rest = (value - top.astype(jnp.float32)).astype(jnp.bfloat16)
                for one, two in ((rest, right_hi), (top, right_lo), (top, right_hi)):
                    total += lax.dot_general(one, two[:, span], NT, preferred_element_type=jnp.float32)
            dst[rows, :] = total

    def place(d, side_y, slot):
        return (((h + d) % far) * 4 + low * 2 + side_y) * slots + slot

    def y_copy(index):
        return pltpu.make_async_remote_copy(
            src_ref=ysend.at[index],
            dst_ref=yrecv.at[index],
            send_sem=y_send.at[index],
            recv_sem=y_recv.at[index],
            device_id=across,
            device_id_type=MESH,
        )

    @pl.loop(0, far * slots)
    def _(index):
        tile(place(index // slots + 1, 1 - y, index % slots), ysend.at[index])
        y_copy(index).start()

    def z_copy(index):
        d = index // slots + 1
        return pltpu.make_async_remote_copy(
            src_ref=zsend.at[index],
            dst_ref=zrecv.at[index],
            send_sem=z_send.at[index],
            recv_sem=z_recv.at[index],
            device_id=(row, ((h + d) % far) * 4 + low * 2 + y),
            device_id_type=MESH,
        )

    hops = (far - 1) * slots

    @pl.loop(0, hops)
    def _(index):
        tile(place(index // slots + 1, y, index % slots), own)
        y_copy(index).wait_recv()
        zsend[index] = own[...] + yrecv[index]
        z_copy(index).start()

    @pl.loop(0, slots)
    def _(slot):
        tile(place(0, y, slot), out.at[slot])

    @pl.loop(0, slots)
    def _(slot):
        y_copy(hops + slot).wait_recv()
        out[slot] = out[slot] + yrecv[hops + slot]

    @pl.loop(0, hops)
    def _(index):
        z_copy(index).wait_recv()
        slot = index % slots
        out[slot] = out[slot] + zrecv[index]

    for slot in range(slots):
        live = table[2, place(0, y, slot)]
        out[slot] = jnp.where(live > 0, out[slot], 0.0)

    for copy in sent:
        copy.wait_send()

    @pl.loop(0, far * slots)
    def _(index):
        y_copy(index).wait_send()

    @pl.loop(0, hops)
    def _(index):
        z_copy(index).wait_send()


def body(panel_rows, owner_slot):
    rows_n = lax.axis_size("row")
    cols_n = lax.axis_size("col")
    slab_rows, depth = panel_rows.shape
    per_group = slab_rows // BLOCK
    blocks = per_group * rows_n
    row_tiles = per_group * (blocks - per_group) + per_group * (per_group + 1) // 2
    slots = (row_tiles + cols_n - 1) // cols_n
    positions = cols_n * slots
    table = jnp.stack([part.astype(jnp.int32) for part in slot_table(owner_slot, lax.axis_index("row"), positions, per_group)])
    chips, far = rows_n // 2, cols_n // 4
    pushes = per_group * ((chips - 1) * 4 + 3) + per_group * (chips - 1)
    tiles = far * slots
    hops = (far - 1) * slots
    summed = pl.pallas_call(
        functools.partial(kernel, rows_n, cols_n, per_group, slots),
        out_shape=jax.ShapeDtypeStruct((slots, BLOCK, BLOCK), jnp.float32),
        in_specs=[pl.BlockSpec(memory_space=pltpu.SMEM), pl.BlockSpec(memory_space=pl.ANY)],
        out_specs=pl.BlockSpec(memory_space=pltpu.VMEM),
        scratch_shapes=[
            pltpu.VMEM((blocks, 2, BLOCK, depth), jnp.float32),
            pltpu.VMEM((tiles, BLOCK, BLOCK), jnp.float32),
            pltpu.VMEM((tiles, BLOCK, BLOCK), jnp.float32),
            pltpu.VMEM((hops, BLOCK, BLOCK), jnp.float32),
            pltpu.VMEM((hops, BLOCK, BLOCK), jnp.float32),
            pltpu.VMEM((BLOCK, BLOCK), jnp.float32),
            pltpu.VMEM((BLOCK, 2 * depth), jnp.bfloat16),
            pltpu.VMEM((BLOCK, 2 * depth), jnp.bfloat16),
            pltpu.SemaphoreType.DMA,
            pltpu.SemaphoreType.DMA((blocks, 2)),
            pltpu.SemaphoreType.DMA((pushes,)),
            pltpu.SemaphoreType.DMA((tiles,)),
            pltpu.SemaphoreType.DMA((tiles,)),
            pltpu.SemaphoreType.DMA((hops,)),
            pltpu.SemaphoreType.DMA((hops,)),
        ],
        compiler_params=pltpu.CompilerParams(
            collective_id=0, has_side_effects=True, vmem_limit_bytes=60 * 2**20
        ),
        cost_estimate=pl.CostEstimate(flops=2 * positions * BLOCK * BLOCK * depth, bytes_accessed=2**22, transcendentals=0),
    )(table, panel_rows.reshape(per_group, BLOCK, depth))
    return summed[None]


def solution(mesh):
    placed = (P("row", "col"), P())
    return jax.shard_map(
        body, mesh=mesh, in_specs=placed, out_specs=P("row", "col", None, None), check_vma=False
    )
```

time: 513 us -> 205 us (0.40)
  waiting for transfers between devices: 435 us -> 0 us
  Pallas kernels: 0 us -> 200 us
  local copies, waits for them, and re-layouts: 31.4 us -> 3.08 us
  loops' own time: 19.6 us -> 0 us
  between operations: 13.4 us -> 0.01 us
  matrix products: 10.3 us -> 0 us
    reduce_scatter x1 -> x0, waiting for transfers between devices: 373 us -> none  [body(): lax.psum_scatter(tile_products(tiles_all, left_block, right_block, is_liv...]
    pallas_call x0 -> x1, Pallas kernels: none -> 200 us  [body(): pl.pallas_call(functools.partial(kernel, rows_n, cols_n, per_group, slots...]
    all_gather x1 -> x0, waiting for transfers between devices: 60.9 us -> none  [body(): gathered = lax.all_gather(panel_rows, 'row', axis=0, tiled=True)]
    another operation x17 -> x0, loops' own time: 19.6 us -> none  [the longest x16 10.4 us: single(): return lax.cond(flag, compute, blank)]
    dynamic_update_slice x16 -> x0, local copies, waits for them, and re-layouts: 17.1 us -> none  [tile_products(): return lax.map(single, (lefts, rights, flags))]
    dynamic_slice x22 -> x0, local copies, waits for them, and re-layouts: 12.7 us -> none  [tile_products(): return lax.map(single, (lefts, rights, flags))]
    dot_general x3 -> x0, matrix products: 10.3 us -> none  [compute(): lax.dot_general(tiles_all[left_one], tiles_all[right_one], (((1,), (1,)),...]
  transfers between devices with their start and end apart: 2 -> 0, of which waited for: 2 -> 0; matrix products, arithmetic and copies ran while one was open for 0% -> 0% of each run, Pallas kernels for 0% -> 0%
where the time goes in v1:
time: 205 us
  Pallas kernels  200 us (98%)
  local copies, waits for them, and re-layouts  3.08 us (2%)
  other arithmetic  2.25 us (1%)
    pallas_call x1, Pallas kernels, body(): pl.pallas_call(functools.partial(kernel, rows_n, cols_n, per_group, slots...  200 us

profile of v1, /device:TPU:0, one launch (start us, length us, event | category | flops | bytes accessed | tf_op | source)
XLA Modules:
  0.0 205.0 jit_solution(11877792718465155507)
XLA Ops:
  0.0 0.1 fusion.2
  0.1 0.8 fusion.1
  0.9 0.8 select_reduce_fusion.1
  1.7 0.6 pad_add_fusion.table
  2.3 199.6 %shard_map.28 = f32[2,512,512]{2,1,0:T(8,128)} custom-call(s32[3,16]{1,0:T(4,128)} %pad_add_fusion.table, f32[2,512,512]{2,1,0:T(8,128)} %bitcast.9), custom_call_target="tpu_custom_call" | custom-call | flops 4294967296 | bytes 4194304 | tf_op jit(solution)/shard_map/pallas_call | solution.py:222
  201.9 3.1 %copy.4 = f32[1,2,512,512]{3,2,1,0:T(8,128)} copy(f32[1,2,512,512]{3,2,1,0:T(8,128)} %bitcast.6) | data formatting | bytes 4194304
  (2 shorter events, 0.0 us)

commit v2 on v0

v2 whole, which is shorter than its diff:
```python
import functools

import jax
import jax.numpy as jnp
from jax import lax
from jax.experimental import pallas as pl
from jax.experimental.pallas import tpu as pltpu
from jax.sharding import PartitionSpec as P

BLOCK = 512
EDGES = (0, 128, 256, 384, 512)
MESH = pl.DeviceIdType.MESH
NT = (((1,), (1,)), ((), ()))


def slot_table(owner_slot, group_id, positions, per_group):
    blocks = owner_slot.shape[0]
    block_row = jnp.arange(blocks, dtype=jnp.int32)[:, None]
    block_col = jnp.arange(blocks, dtype=jnp.int32)[None, :]
    inside = (block_row // per_group == group_id) & (block_col <= block_row)
    wanted = jnp.arange(positions, dtype=jnp.int32)[:, None, None]
    matched = inside[None] & (owner_slot[None] == wanted)
    is_live = jnp.any(matched, axis=(1, 2))
    left_block = jnp.sum(jnp.where(matched, block_row[None], 0), axis=(1, 2))
    right_block = jnp.sum(jnp.where(matched, block_col[None], 0), axis=(1, 2))
    return (left_block, right_block, is_live)


STAGES = len(EDGES) - 1
PIECES = []
for stage in range(STAGES):
    PIECES.append((stage, EDGES[stage], EDGES[stage + 1], 0, EDGES[stage + 1]))
    if stage:
        PIECES.append((stage, 0, EDGES[stage], EDGES[stage], EDGES[stage + 1]))


def kernel(rows_n, cols_n, per_group, slots, table, panel, out, *scratch):
    count = len(PIECES)
    scratch = list(scratch)

    def take(number):
        taken = scratch[:number]
        del scratch[:number]
        return taken

    held = take(STAGES)
    ysend, yrecv, zsend, zrecv = take(count), take(count), take(count), take(count)
    right_hi, right_lo, local_sem, load_recv, load_send, y_send, y_recv, z_send, z_recv = scratch
    row, col = lax.axis_index("row"), lax.axis_index("col")
    chips = rows_n // 2
    far = cols_n // 4
    x, core = row // 2, row % 2
    h, low, y = col // 4, (col // 2) % 2, col % 2
    sibling = (row + 1 - 2 * core, col)
    pair = (row, h * 4 + (1 - low) * 2 + y)
    across = (row, h * 4 + low * 2 + 1 - y)
    beside = [(((x + d) % chips) * 2 + core, col) for d in range(1, chips)]
    ahead = [(row, ((h + d) % far) * 4 + low * 2 + y) for d in range(1, far)]
    partners = [sibling, pair, across] + beside + ahead

    fetches = []
    for stage in range(STAGES):
        fetch = pltpu.make_async_copy(
            panel.at[:, pl.ds(EDGES[stage], EDGES[stage + 1] - EDGES[stage])],
            held[stage].at[pl.ds(row * per_group, per_group), low],
            local_sem.at[stage],
        )
        fetch.start()
        fetches.append(fetch)
    barrier = pltpu.get_barrier_semaphore()
    for device in partners:
        pl.semaphore_signal(barrier, inc=1, device_id=device, device_id_type=MESH)
    pl.semaphore_wait(barrier, len(partners))

    sent = []

    def push(stage, group, side, half, device):
        block = group * per_group + half
        copy = pltpu.make_async_remote_copy(
            src_ref=held[stage].at[block, side],
            dst_ref=held[stage].at[block, side],
            send_sem=load_send.at[len(sent)],
            recv_sem=load_recv.at[stage, block, side],
            device_id=device,
            device_id_type=MESH,
        )
        copy.start()
        sent.append(copy)

    def arrive(stage, group, side, half):
        block = group * per_group + half
        pltpu.make_async_remote_copy(
            src_ref=held[stage].at[block, side],
            dst_ref=held[stage].at[block, side],
            send_sem=load_send.at[0],
            recv_sem=load_recv.at[stage, block, side],
            device_id=sibling,
            device_id_type=MESH,
        ).wait_recv()

    cut = per_group // 2
    ups, downs = list(range(cut)), list(range(cut, per_group))
    others = [((x + chips - d) % chips) * 2 + core for d in range(1, chips)]

    def first(stage):
        fetches[stage].wait()
        for half in ups + downs:
            for device in beside:
                push(stage, row, low, half, device)
        for half in downs + ups:
            push(stage, row, low, half, pair)
        for half in ups + downs:
            push(stage, row, low, half, sibling)

    def second(stage):
        for group in others:
            for half in ups:
                arrive(stage, group, low, half)
                push(stage, group, low, half, pair)
                push(stage, group, low, half, sibling)
        for half in downs:
            arrive(stage, row, 1 - low, half)
            for device in beside:
                push(stage, row, 1 - low, half, device)
            push(stage, row, 1 - low, half, sibling)

    def third(stage):
        for group in others:
            for half in downs:
                arrive(stage, group, low, half)
                push(stage, group, low, half, sibling)
        for half in ups:
            arrive(stage, row, 1 - low, half)
            push(stage, row, 1 - low, half, sibling)
        for group in others:
            for half in ups + downs:
                arrive(stage, group, 1 - low, half)
                push(stage, group, 1 - low, half, sibling)
        for d in range(chips):
            group = ((x + d) % chips) * 2 + 1 - core
            for side in range(2):
                for half in range(per_group):
                    arrive(stage, group, side, half)

    depth = held[0].shape[-1]

    def split(value):
        top = value.astype(jnp.bfloat16)
        return top, (value - top.astype(jnp.float32)).astype(jnp.bfloat16)

    def strips(stage, position, emit, fresh=0):
        left, right = table[0, position], table[1, position]
        for part in range(fresh, stage + 1):
            for side in range(2):
                where = (slice(EDGES[part], EDGES[part + 1]), slice(side * depth, (side + 1) * depth))
                right_hi[where], right_lo[where] = split(held[part][right, side])

        def product(part, begin, end):
            total = None
            for side in range(2):
                span = slice(side * depth, (side + 1) * depth)
                top, rest = split(held[part][left, side])
                for one, two in ((rest, right_hi), (top, right_lo), (top, right_hi)):
                    term = lax.dot_general(one, two[begin:end, span], NT, preferred_element_type=jnp.float32)
                    total = term if total is None else total + term
            return total

        for number, (own_stage, r0, r1, c0, c1) in enumerate(PIECES):
            if own_stage == stage:
                for part in range(STAGES):
                    if r0 <= EDGES[part] < r1:
                        emit(number, EDGES[part] - r0, EDGES[part + 1] - r0, product(part, c0, c1))

    def numbers(stage):
        return [number for number, piece in enumerate(PIECES) if piece[0] == stage]

    def place(d, side_y, slot):
        return (((h + d) % far) * 4 + low * 2 + side_y) * slots + slot

    def y_copy(number, index):
        return pltpu.make_async_remote_copy(
            src_ref=ysend[number].at[index],
            dst_ref=yrecv[number].at[index],
            send_sem=y_send.at[number, index],
            recv_sem=y_recv.at[number, index],
            device_id=across,
            device_id_type=MESH,
        )

    def z_copy(number, index):
        return pltpu.make_async_remote_copy(
            src_ref=zsend[number].at[index],
            dst_ref=zrecv[number].at[index],
            send_sem=z_send.at[number, index],
            recv_sem=z_recv.at[number, index],
            device_id=(row, ((h + index // slots + 1) % far) * 4 + low * 2 + y),
            device_id_type=MESH,
        )

    tiles, hops = far * slots, (far - 1) * slots

    def y_work(stage):
        @pl.loop(0, tiles)
        def _(index):
            def emit(number, begin, end, value):
                ysend[number][index, begin:end, :] = value

            strips(stage, place(index // slots + 1, 1 - y, index % slots), emit)
            for number in numbers(stage):
                y_copy(number, index).start()

    def z_work(stage):
        @pl.loop(0, hops)
        def _(index):
            def emit(number, begin, end, value):
                zsend[number][index, begin:end, :] = value

            strips(stage, place(index // slots + 1, y, index % slots), emit)
            for number in numbers(stage):
                y_copy(number, index).wait_recv()
                zsend[number][index] += yrecv[number][index]
                z_copy(number, index).start()

    first(0)
    for stage in range(STAGES):
        second(stage)
        if stage + 1 < STAGES:
            first(stage + 1)
        if stage:
            z_work(stage - 1)
        third(stage)
        y_work(stage)
    z_work(STAGES - 1)

    @pl.loop(0, slots)
    def _(slot):
        def emit(number, begin, end, value):
            _, r0, _, c0, c1 = PIECES[number]
            out[slot, r0 + begin:r0 + end, c0:c1] = value

        for stage in range(STAGES):
            strips(stage, place(0, y, slot), emit, stage)
        for number, (_, r0, r1, c0, c1) in enumerate(PIECES):
            y_copy(number, hops + slot).wait_recv()
            out[slot, r0:r1, c0:c1] += yrecv[number][hops + slot]

    for number, (_, r0, r1, c0, c1) in enumerate(PIECES):
        @pl.loop(0, hops)
        def _(index):
            z_copy(number, index).wait_recv()
            slot = index % slots
            out[slot, r0:r1, c0:c1] += zrecv[number][index]

    for slot in range(slots):
        live = table[2, place(0, y, slot)]
        out[slot] = jnp.where(live > 0, out[slot], 0.0)

    for copy in sent:
        copy.wait_send()
    for number in range(count):
        @pl.loop(0, tiles)
        def _(index):
            y_copy(number, index).wait_send()

        @pl.loop(0, hops)
        def _(index):
            z_copy(number, index).wait_send()


def body(panel_rows, owner_slot):
    rows_n = lax.axis_size("row")
    cols_n = lax.axis_size("col")
    slab_rows, depth = panel_rows.shape
    per_group = slab_rows // BLOCK
    blocks = per_group * rows_n
    row_tiles = per_group * (blocks - per_group) + per_group * (per_group + 1) // 2
    slots = (row_tiles + cols_n - 1) // cols_n
    positions = cols_n * slots
    table = jnp.stack([part.astype(jnp.int32) for part in slot_table(owner_slot, lax.axis_index("row"), positions, per_group)])
    chips, far = rows_n // 2, cols_n // 4
    pushes = per_group * ((chips - 1) * 4 + 3) + per_group * (chips - 1)
    tiles = far * slots
    hops = (far - 1) * slots
    summed = pl.pallas_call(
        functools.partial(kernel, rows_n, cols_n, per_group, slots),
        out_shape=jax.ShapeDtypeStruct((slots, BLOCK, BLOCK), jnp.float32),
        in_specs=[pl.BlockSpec(memory_space=pltpu.SMEM), pl.BlockSpec(memory_space=pl.ANY)],
        out_specs=pl.BlockSpec(memory_space=pltpu.VMEM),
        scratch_shapes=[pltpu.VMEM((blocks, 2, EDGES[stage + 1] - EDGES[stage], depth), jnp.float32) for stage in range(STAGES)]
        + [
            pltpu.VMEM((number, r1 - r0, c1 - c0), jnp.float32)
            for number in (tiles, tiles, hops, hops)
            for _, r0, r1, c0, c1 in PIECES
        ]
        + [
            pltpu.VMEM((BLOCK, 2 * depth), jnp.bfloat16),
            pltpu.VMEM((BLOCK, 2 * depth), jnp.bfloat16),
            pltpu.SemaphoreType.DMA((STAGES,)),
            pltpu.SemaphoreType.DMA((STAGES, blocks, 2)),
            pltpu.SemaphoreType.DMA((STAGES * pushes,)),
            pltpu.SemaphoreType.DMA((len(PIECES), tiles)),
            pltpu.SemaphoreType.DMA((len(PIECES), tiles)),
            pltpu.SemaphoreType.DMA((len(PIECES), hops)),
            pltpu.SemaphoreType.DMA((len(PIECES), hops)),
        ],
        compiler_params=pltpu.CompilerParams(
            collective_id=0, has_side_effects=True, vmem_limit_bytes=60 * 2**20
        ),
        cost_estimate=pl.CostEstimate(flops=2 * positions * BLOCK * BLOCK * depth, bytes_accessed=2**22, transcendentals=0),
    )(table, panel_rows.reshape(per_group, BLOCK, depth))
    return summed[None]


def solution(mesh):
    placed = (P("row", "col"), P())
    return jax.shard_map(
        body, mesh=mesh, in_specs=placed, out_specs=P("row", "col", None, None), check_vma=False
    )
```

time: 513 us -> 156 us (0.30)
  waiting for transfers between devices: 435 us -> 0 us
  Pallas kernels: 0 us -> 150 us
  local copies, waits for them, and re-layouts: 31.4 us -> 3.08 us
  loops' own time: 19.6 us -> 0 us
  between operations: 13.4 us -> 0.01 us
  matrix products: 10.3 us -> 0 us
    reduce_scatter x1 -> x0, waiting for transfers between devices: 373 us -> none  [body(): lax.psum_scatter(tile_products(tiles_all, left_block, right_block, is_liv...]
    pallas_call x0 -> x1, Pallas kernels: none -> 150 us  [body(): pl.pallas_call(functools.partial(kernel, rows_n, cols_n, per_group, slots...]
    all_gather x1 -> x0, waiting for transfers between devices: 60.9 us -> none  [body(): gathered = lax.all_gather(panel_rows, 'row', axis=0, tiled=True)]
    another operation x17 -> x0, loops' own time: 19.6 us -> none  [the longest x16 10.4 us: single(): return lax.cond(flag, compute, blank)]
    dynamic_update_slice x16 -> x0, local copies, waits for them, and re-layouts: 17.1 us -> none  [tile_products(): return lax.map(single, (lefts, rights, flags))]
    dynamic_slice x22 -> x0, local copies, waits for them, and re-layouts: 12.7 us -> none  [tile_products(): return lax.map(single, (lefts, rights, flags))]
    dot_general x3 -> x0, matrix products: 10.3 us -> none  [compute(): lax.dot_general(tiles_all[left_one], tiles_all[right_one], (((1,), (1,)),...]
  transfers between devices with their start and end apart: 2 -> 0, of which waited for: 2 -> 0; matrix products, arithmetic and copies ran while one was open for 0% -> 0% of each run, Pallas kernels for 0% -> 0%
where the time goes in v2:
time: 156 us
  Pallas kernels  150 us (96%)
  local copies, waits for them, and re-layouts  3.08 us (2%)
  other arithmetic  2.25 us (1%)
    pallas_call x1, Pallas kernels, body(): pl.pallas_call(functools.partial(kernel, rows_n, cols_n, per_group, slots...  150 us

profile of v2, /device:TPU:0, one launch (start us, length us, event | category | flops | bytes accessed | tf_op | source)
XLA Modules:
  0.0 155.6 jit_solution(4358490813730405761)
XLA Ops:
  0.0 0.1 fusion.2
  0.1 0.8 fusion.1
  0.9 0.8 select_reduce_fusion.1
  1.7 0.6 pad_add_fusion.table
  2.3 150.2 %shard_map.28 = f32[2,512,512]{2,1,0:T(8,128)} custom-call(s32[3,16]{1,0:T(4,128)} %pad_add_fusion.table, f32[2,512,512]{2,1,0:T(8,128)} %bitcast.9), custom_call_target="tpu_custom_call" | custom-call | flops 4294967296 | bytes 4194304 | tf_op jit(solution)/shard_map/pallas_call | solution.py:284
  152.5 3.1 %copy.4 = f32[1,2,512,512]{3,2,1,0:T(8,128)} copy(f32[1,2,512,512]{3,2,1,0:T(8,128)} %bitcast.6) | data formatting | bytes 4194304
  (2 shorter events, 0.0 us)
